TPU v7x, 32 devices: a whole 2x2x4 slice. The times are simulated.
32 devices in a mesh: gx: 4 (over y, x), gy: 2 (over core), gz: 4 (over z).
Axes of the slice: x: 2, y: 2, z: 4, core: 2. Of those that a mesh axis runs over, the one named last changes fastest.
Arguments:
- gradient: bfloat16 [32, 32, 16, 512], P(None, 'gx', 'gy', 'gz'), may hold values from -6 to 6
- noise_draw: bfloat16 [32, 32, 16, 512], P(None, 'gx', 'gy', 'gz'), may hold values from -6 to 6
- current: float32 [32, 32, 16, 512], P(None, 'gx', 'gy', 'gz'), may hold values from -6 to 6
- eigvectors: bfloat16 [32, 16, 512, 512], P('gx', 'gy', 'gz'), may hold values from -0.125 to 0.125
- eigvalues: float32 [512], replicated, may hold values from 0.05 to 50
- reaction: float32 [32, 16, 512], P('gx', 'gy', 'gz'), may hold values from 0.25 to 4
Outputs:
- proposal: float32 [32, 32, 16, 512], P(None, 'gx', 'gy', 'gz')
All inputs are finite; a program needn't handle non-finite values.
Results may differ from a plain program's by a relative error of at most 0.00031.
Values sent between devices are 32-bit elements; how exact they have to be, the bound alone decides.
A program may use at most 64 MiB of HBM per device.

v0:
```python
import functools

import jax
import jax.numpy as jnp
from jax import lax
from jax.experimental import pallas as pl
from jax.experimental.pallas import tpu as pltpu
from jax.sharding import PartitionSpec as P

SWEEPS = 4
GROUPS = 2
MESH = pl.DeviceIdType.MESH
AXES = ("gx", "gy", "gz")


def kernel(
    sizes, shape, g_h, n_h, cur_h, eig_h, ev_ref, rea_h, out_h,
    eig_v, gb, nb, gf, nf, cur_v, rdv, lhs, src, fields, zout, zin,
    part, got1, got2, full, load_sem, out_sem,
    send1, recv1, send2, recv2, send3, recv3, hsend, hrecv,
):
    C, X, Y, Z, R = shape
    NX, NY, NZ = sizes
    G = src.shape[0]
    CG = C // G
    XY = X * Y
    S = SWEEPS - 1
    PL = NX * NY
    rows = part.shape[1]
    pos = {a: lax.axis_index(a) for a in AXES}
    count = dict(zip(AXES, sizes))
    me_p = pos["gx"] * NY + pos["gy"]
    me_z = pos["gz"]

    loads = [
        pltpu.make_async_copy(g_h, gb, load_sem.at[0]),
        pltpu.make_async_copy(n_h, nb, load_sem.at[1]),
        pltpu.make_async_copy(rea_h, rdv, load_sem.at[2]),
        pltpu.make_async_copy(cur_h, cur_v, load_sem.at[3]),
    ]
    eig_loads = [
        pltpu.make_async_copy(eig_h.at[x], eig_v.at[x], load_sem.at[4 + x]) for x in range(X)
    ]
    for c in loads[:3] + eig_loads + loads[3:]:
        c.start()

    barrier = pltpu.get_barrier_semaphore()

    def plane_peer(d):
        q = lax.rem(me_p + d, PL)
        return {"gx": q // NY, "gy": lax.rem(q, NY)}, q

    for d in range(1, PL):
        pl.semaphore_signal(barrier, inc=1, device_id=plane_peer(d)[0], device_id_type=MESH)
    for d in range(1, NZ):
        pl.semaphore_signal(
            barrier, inc=1, device_id={"gz": lax.rem(me_z + d, NZ)}, device_id_type=MESH
        )

    zeros = jnp.zeros((Y, CG, Z), jnp.float32)
    zerosy = jnp.zeros((X, CG, Z), jnp.float32)

    def fill(cond, fn):
        if cond is True:
            fn()
        else:
            pl.when(cond)(fn)

    def low_edge(a):
        return True if count[a] == 1 else pos[a] == 0

    def high_edge(a):
        return True if count[a] == 1 else pos[a] == count[a] - 1

    for k in range(S):
        for g in range(G):
            def x0(k=k, g=g):
                fields[k, g, 0, 1 : Y + 1] = zeros
            def x1(k=k, g=g):
                fields[k, g, X + 1, 1 : Y + 1] = zeros
            def y0(k=k, g=g):
                fields[k, g, 1 : X + 1, 0] = zerosy
            def y1(k=k, g=g):
                fields[k, g, 1 : X + 1, Y + 1] = zerosy
            def z0(k=k, g=g):
                zin[k, g, 0] = jnp.zeros((CG, Z), jnp.float32)
            def z1(k=k, g=g):
                zin[k, g, 1] = jnp.zeros((CG, Z), jnp.float32)
            fill(low_edge("gx"), x0)
            fill(high_edge("gx"), x1)
            fill(low_edge("gy"), y0)
            fill(high_edge("gy"), y1)
            fill(low_edge("gz"), z0)
            fill(high_edge("gz"), z1)

    loads[0].wait()
    loads[1].wait()
    loads[2].wait()
    rdv[...] = 1.0 / (rdv[...] + 6.0)
    CH = XY
    @pl.loop(0, C)
    def _(c):
        r = pl.ds(pl.multiple_of(c * CH, CH), CH)
        gf[r, :] = gb[r, :].astype(jnp.float32)
        nf[r, :] = nb[r, :].astype(jnp.float32)

    @pl.loop(0, X)
    def _(x):
        for y in range(Y):
            at = pl.ds(x * Y + y, C, stride=XY)
            gv = gf[at, :]
            nv = nf[at, :]
            lhs[x, 0:C, y * Z : (y + 1) * Z] = gv.astype(jnp.bfloat16)
            lhs[x, C : 2 * C, y * Z : (y + 1) * Z] = nv.astype(jnp.bfloat16)
            s = -0.5 * gv + nv
            for g in range(G):
                src[g, x, y] = s[g * CG : (g + 1) * CG]

    acc = None
    for x in range(X):
        eig_loads[x].wait()
        term = jnp.dot(lhs[x], eig_v[x], preferred_element_type=jnp.float32)
        acc = term if acc is None else acc + term
    ev = ev_ref[...]
    damp = ev / (ev + 1.0)
    root_damp = 1.0 - 1.0 / jnp.sqrt(1.0 + ev)
    comb = (0.5 * damp) * acc[:C] - root_damp * acc[C:]
    RT = R // 128
    tiles = [(c, r) for c in range(C // 8) for r in range(RT)]
    for t, (c, r) in enumerate(tiles):
        tile = comb[c * 8 : (c + 1) * 8, r * 128 : (r + 1) * 128]
        if rows >= 8:
            o = (t * 8) % rows
            part[(t * 8) // rows, o : o + 8, :] = tile
        else:
            for j in range(8 // rows):
                part[(t * 8) // rows + j] = tile[j * rows : (j + 1) * rows]

    pl.semaphore_wait(barrier, PL - 1 + NZ - 1)

    copies1 = []
    for d in range(1, PL):
        dev, q = plane_peer(d)
        copies1.append(pltpu.make_async_remote_copy(
            src_ref=part.at[q], dst_ref=got1.at[d],
            send_sem=send1.at[d], recv_sem=recv1.at[d],
            device_id=dev, device_id_type=MESH))
    for c in copies1:
        c.start()
    total = part[me_p]
    for d in range(1, PL):
        copies1[d - 1].wait_recv()
        total = total + got1[d]
    got2[me_z] = total
    copies2 = []
    for d in range(1, NZ):
        copies2.append(pltpu.make_async_remote_copy(
            src_ref=got2.at[me_z], dst_ref=got2.at[me_z],
            send_sem=send2.at[d], recv_sem=recv2.at[d],
            device_id={"gz": lax.rem(me_z + d, NZ)}, device_id_type=MESH))
    for c in copies2:
        c.start()
    for c in copies2:
        c.wait_recv()
    total = got2[0]
    for j in range(1, NZ):
        total = total + got2[j]
    full[me_p] = total
    copies3 = []
    for d in range(1, PL):
        copies3.append(pltpu.make_async_remote_copy(
            src_ref=full.at[me_p], dst_ref=full.at[me_p],
            send_sem=send3.at[d], recv_sem=recv3.at[d],
            device_id=plane_peer(d)[0], device_id_type=MESH))
    for c in copies3:
        c.start()
    for c in copies3:
        c.wait_recv()
    bands = []
    for c in range(C // 8):
        band = []
        for r in range(RT):
            t = c * RT + r
            if rows >= 8:
                o = (t * 8) % rows
                band.append(full[(t * 8) // rows, o : o + 8, :])
            else:
                band.append(jnp.concatenate(
                    [full[(t * 8) // rows + j] for j in range(8 // rows)], 0))
        bands.append(jnp.concatenate(band, 1))
    coef = jnp.concatenate(bands, 0).astype(jnp.bfloat16)

    lane = lax.broadcasted_iota(jnp.int32, (CG, Z), 1)

    def halo(k, g, axis, sign):
        i = AXES.index(axis) * 2 + (sign > 0)
        if axis == "gx":
            s = fields.at[k, g, X if sign > 0 else 1, 1 : Y + 1]
            d = fields.at[k, g, 0 if sign > 0 else X + 1, 1 : Y + 1]
        elif axis == "gy":
            s = fields.at[k, g, 1 : X + 1, Y if sign > 0 else 1]
            d = fields.at[k, g, 1 : X + 1, 0 if sign > 0 else Y + 1]
        else:
            s = zout.at[k, g, 1 if sign > 0 else 0]
            d = zin.at[k, g, 0 if sign > 0 else 1]
        n = count[axis]
        to = lax.rem(pos[axis] + (sign + n), n)
        copy = pltpu.make_async_remote_copy(
            src_ref=s, dst_ref=d, send_sem=hsend.at[k, g, i], recv_sem=hrecv.at[k, g, i],
            device_id={axis: to}, device_id_type=MESH)
        up, down = pos[axis] < n - 1, pos[axis] > 0
        return copy, (up if sign > 0 else down), (down if sign > 0 else up)

    ways = [(a, s) for a in AXES if count[a] > 1 for s in (-1, 1)]

    def send(k, g, axes):
        for a, s in ways:
            if a in axes:
                copy, out, _ = halo(k, g, a, s)
                pl.when(out)(copy.start)

    def wait_halos(k, g):
        for a, s in ways:
            copy, _, come = halo(k, g, a, s)
            pl.when(come)(copy.wait_recv)

    def wait_sends(k, g):
        for a, s in ways:
            copy, out, _ = halo(k, g, a, s)
            pl.when(out)(copy.wait_send)

    def packed(x, y, f, low, high):
        l = x * Y + y
        low = jnp.where(lane == l, pltpu.roll(f, l, 1), low)
        high = jnp.where(lane == l, pltpu.roll(f, l + 1, 1), high)
        return low, high

    nothing = jnp.zeros((CG, Z), jnp.float32)

    def first(x, carry):
        corr = lax.dot_general(
            coef, eig_v[x], (((1,), (1,)), ((), ())), preferred_element_type=jnp.float32)
        rdx = rdv[x]
        carry = list(carry)
        for y in range(Y):
            for g in range(G):
                s = src[g, x, y] + corr[g * CG : (g + 1) * CG, y * Z : (y + 1) * Z]
                src[g, x, y] = s
                f = s * rdx[y : y + 1]
                fields[0, g, x + 1, y + 1] = f
                carry[2 * g], carry[2 * g + 1] = packed(x, y, f, carry[2 * g], carry[2 * g + 1])
        return tuple(carry)

    carry = first(0, (nothing,) * (2 * G))
    carry = first(X - 1, carry)
    for g in range(G):
        send(0, g, ("gx",))
    carry = lax.fori_loop(1, X - 1, first, carry)
    for g in range(G):
        zout[0, g, 0] = carry[2 * g]
        zout[0, g, 1] = carry[2 * g + 1]
    for g in range(G):
        send(0, g, ("gz", "gy"))

    loads[3].wait()
    outs = []
    for k in range(S):
        for g in range(G):
            wait_halos(k, g)
            zlo = zin[k, g, 0]
            zhi = zin[k, g, 1]

            def step(x, carry, k=k, g=g):
                rdx = rdv[x]
                low, high, zlo, zhi = carry
                low = pltpu.roll(low, Z - Y, 1)
                high = pltpu.roll(high, Z - Y, 1)
                done = []
                for y in range(Y):
                    f = fields[k, g, x + 1, y + 1]
                    t = fields[k, g, x + 2, y + 1] + fields[k, g, x, y + 1]
                    t = t + (fields[k, g, x + 1, y + 2] + fields[k, g, x + 1, y])
                    up = jnp.where(lane == Z - 1, pltpu.roll(zhi, Z - 1 - y, 1), pltpu.roll(f, Z - 1, 1))
                    down = jnp.where(lane == 0, pltpu.roll(zlo, (Z - y) % Z, 1), pltpu.roll(f, 1, 1))
                    v = (src[g, x, y] + (t + (up + down))) * rdx[y : y + 1]
                    if k < S - 1:
                        m = (X - 1) * Y + y
                        low = jnp.where(lane == m, pltpu.roll(v, m, 1), low)
                        high = jnp.where(lane == m, pltpu.roll(v, m + 1, 1), high)
                    else:
                        v = v + cur_v[pl.ds(g * CG * XY + x * Y + y, CG, stride=XY), :]
                    done.append(v)
                for y, v in enumerate(done):
                    if k < S - 1:
                        fields[k + 1, g, x + 1, y + 1] = v
                    else:
                        cur_v[pl.ds(g * CG * XY + x * Y + y, CG, stride=XY), :] = v
                return low, high, pltpu.roll(zlo, Z - Y, 1), pltpu.roll(zhi, Z - Y, 1)

            low, high, _, _ = lax.fori_loop(0, X, step, (nothing, nothing, zlo, zhi))
            if k < S - 1:
                zout[k + 1, g, 0] = low
                zout[k + 1, g, 1] = high
                send(k + 1, g, AXES)
            else:
                r = pl.ds(g * CG * XY, CG * XY)
                c = pltpu.make_async_copy(cur_v.at[r], out_h.at[r], out_sem.at[g])
                c.start()
                outs.append(c)
    for c in copies1 + copies2 + copies3:
        c.wait_send()
    for k in range(S):
        for g in range(G):
            wait_sends(k, g)
    for c in outs:
        c.wait()


def body(sizes, gradient, noise_draw, current, eigvectors, eigvalues, reaction):
    C, X, Y, Z = gradient.shape
    R = eigvectors.shape[3]
    NX, NY, NZ = sizes
    PL = NX * NY
    G = GROUPS
    CG = C // G
    S = SWEEPS - 1
    XY = X * Y
    f32, bf16 = jnp.float32, jnp.bfloat16
    rows = C * R // 128 // PL
    any_space = pl.BlockSpec(memory_space=pl.ANY)
    dma = pltpu.SemaphoreType.DMA
    out = pl.pallas_call(
        functools.partial(kernel, sizes, (C, X, Y, Z, R)),
        out_shape=jax.ShapeDtypeStruct((C * XY, Z), f32),
        in_specs=[any_space] * 4 + [pl.BlockSpec(memory_space=pltpu.VMEM), any_space],
        out_specs=any_space,
        scratch_shapes=[
            pltpu.VMEM((X, Y * Z, R), bf16),
            pltpu.VMEM((C * XY, Z), bf16),
            pltpu.VMEM((C * XY, Z), bf16),
            pltpu.VMEM((C * XY, Z), f32),
            pltpu.VMEM((C * XY, Z), f32),
            pltpu.VMEM((C * XY, Z), f32),
            pltpu.VMEM((X, Y, Z), f32),
            pltpu.VMEM((X, 2 * C, Y * Z), bf16),
            pltpu.VMEM((G, X, Y, CG, Z), f32),
            pltpu.VMEM((S, G, X + 2, Y + 2, CG, Z), f32),
            pltpu.VMEM((S, G, 2, CG, Z), f32),
            pltpu.VMEM((S, G, 2, CG, Z), f32),
            pltpu.VMEM((PL, rows, 128), f32),
            pltpu.VMEM((PL, rows, 128), f32),
            pltpu.VMEM((NZ, rows, 128), f32),
            pltpu.VMEM((PL, rows, 128), f32),
            dma((4 + X,)),
            dma((G,)),
            dma((PL,)), dma((PL,)),
            dma((NZ,)), dma((NZ,)),
            dma((PL,)), dma((PL,)),
            dma((S, G, 6)), dma((S, G, 6)),
        ],
        compiler_params=pltpu.CompilerParams(
            collective_id=0, has_side_effects=True, vmem_limit_bytes=67043328
        ),
    )(
        gradient.reshape(C * XY, Z),
        noise_draw.reshape(C * XY, Z),
        current.reshape(C * XY, Z),
        eigvectors.reshape(X, Y * Z, R),
        eigvalues.reshape(1, R),
        reaction,
    )
    return out.reshape(current.shape)


def solution(mesh):
    return jax.shard_map(
        functools.partial(body, tuple(mesh.shape[a] for a in AXES)),
        mesh=mesh,
        in_specs=(
            P(None, "gx", "gy", "gz"),
            P(None, "gx", "gy", "gz"),
            P(None, "gx", "gy", "gz"),
            P("gx", "gy", "gz", None),
            P(),
            P("gx", "gy", "gz"),
        ),
        out_specs=P(None, "gx", "gy", "gz"),
        check_vma=False,
    )
```

profile of v0, /device:TPU:0, one launch (start us, length us, event | category | flops | bytes accessed | tf_op | source)
XLA Modules:
  0.0 44.7 jit_solution(9632977238318096339)
XLA Ops:
  0.0 42.4 %shard_map.64 = f32[2048,128]{1,0:T(8,128)} custom-call(bf16[2048,128]{1,0:T(8,128)(2,1)} %bitcast.9, bf16[2048,128]{1,0:T(8,128)(2,1)} %bitcast.10, f32[2048,128]{1,0:T(8,128)} %bitcast.8, bf16[8,1024,512]{2,1,0:T(8,128)(2,1)} %bitcast.6, f32[1,512]{1,0:T(1,128)} %bitcast.11, f32[8,8,128]{2,1,0:T(8,128)} %rea_h.1), custom_call_target="tpu_custom_call" | custom-call | tf_op jit(solution)/shard_map/pallas_call | solution.py:332
  42.4 2.3 %copy.8 = f32[32,8,8,128]{3,2,1,0:T(8,128)} copy(f32[32,8,8,128]{3,2,1,0:T(8,128)} %bitcast.7) | data formatting | bytes 2097152
where the time goes:
time: 44.9 us; the launch traced here: 44.7 us
  Pallas kernels  42.4 us (94%)
  local copies, waits for them, and re-layouts  2.31 us (5%)
    pallas_call x1, Pallas kernels, body(): pl.pallas_call(functools.partial(kernel, sizes, (C, X, Y, Z, R)), out_sha...  42.4 us
    unnamed x1, local copies, waits for them, and re-layouts  2.31 us

commit v1 on v0

v1 whole, which is shorter than its diff:
```python
import functools

import jax
import jax.numpy as jnp
from jax import lax
from jax.experimental import pallas as pl
from jax.experimental.pallas import tpu as pltpu
from jax.sharding import PartitionSpec as P

SWEEPS = 4
GROUPS = 4
LEFT = 65536
RELAYED = ((2, 3), (2, 3), ())
ORDER = (
    ("F2", "F3", "E0", "E1", "I0", "I1", "E2", "I2", "E3", "I3"),
    ("F2", "F3", "I0", "E0", "I1", "E1", "I2", "E2", "I3", "E3"),
    ("F2", "F3", "I0", "E0", "I1", "E1", "I2", "E2", "I3", "E3"),
)
MESH = pl.DeviceIdType.MESH
AXES = ("gx", "gy", "gz")


def pitch_of(rows):
    return rows + 8 if (rows // 8) % 2 == 0 else rows


def kernel(
    sizes, shape, g_h, n_h, cur_h, eig_h, ev_ref, rea_h, out_v,
    eig_v, gb, nb, gf, nf, cur_v, rdv, src, fields, zout, zin, relay,
    part, got1, got2, full, load_sem,
    send1, recv1, send2, recv2, send3, recv3, hsend, hrecv, rsend, rrecv,
):
    C, X, Y, Z, R = shape
    NX, NY, NZ = sizes
    G = src.shape[0]
    CG = C // G
    XY = X * Y
    PT = pitch_of(XY)
    S = SWEEPS - 1
    PL = NX * NY
    rows = part.shape[1]
    pos = {a: lax.axis_index(a) for a in AXES}
    count = dict(zip(AXES, sizes))
    me_p = pos["gx"] * NY + pos["gy"]
    me_z = pos["gz"]

    loads = [
        pltpu.make_async_copy(g_h, gb, load_sem.at[0]),
        pltpu.make_async_copy(n_h, nb, load_sem.at[1]),
        pltpu.make_async_copy(rea_h, rdv, load_sem.at[2]),
    ]
    eig_loads = [
        pltpu.make_async_copy(eig_h.at[x], eig_v.at[x], load_sem.at[4 + x]) for x in range(X)
    ]
    for c in loads + eig_loads:
        c.start()

    @pl.loop(0, C)
    def _(c):
        a = pl.ds(pl.multiple_of(c * XY, 8), XY)
        b = pl.ds(pl.multiple_of(c * PT, 8), XY)
        pltpu.make_async_copy(cur_h.at[a], cur_v.at[b], load_sem.at[3]).start()

    barrier = pltpu.get_barrier_semaphore()

    def plane_peer(d):
        q = lax.rem(me_p + d, PL)
        return {"gx": q // NY, "gy": lax.rem(q, NY)}, q

    for d in range(1, PL):
        pl.semaphore_signal(barrier, inc=1, device_id=plane_peer(d)[0], device_id_type=MESH)
    for d in range(1, NZ):
        pl.semaphore_signal(
            barrier, inc=1, device_id={"gz": lax.rem(me_z + d, NZ)}, device_id_type=MESH
        )

    zeros = jnp.zeros((Y, CG, Z), jnp.float32)
    zerosy = jnp.zeros((X, CG, Z), jnp.float32)

    def fill(cond, fn):
        if cond is True:
            fn()
        else:
            pl.when(cond)(fn)

    def low_edge(a):
        return True if count[a] == 1 else pos[a] == 0

    def high_edge(a):
        return True if count[a] == 1 else pos[a] == count[a] - 1

    def fills():
        def x0():
            for k in range(S):
                for g in range(G):
                    fields[k, g, 0, 1 : Y + 1] = zeros
        def x1():
            for k in range(S):
                for g in range(G):
                    fields[k, g, X + 1, 1 : Y + 1] = zeros
        def y0():
            for k in range(S):
                for g in range(G):
                    fields[k, g, 1 : X + 1, 0] = zerosy
        def y1():
            for k in range(S):
                for g in range(G):
                    fields[k, g, 1 : X + 1, Y + 1] = zerosy
        def z0():
            for k in range(S):
                for g in range(G):
                    zin[k, g, 0] = jnp.zeros((CG, Z), jnp.float32)
        def z1():
            for k in range(S):
                for g in range(G):
                    zin[k, g, 1] = jnp.zeros((CG, Z), jnp.float32)
        fill(low_edge("gx"), x0)
        fill(high_edge("gx"), x1)
        fill(low_edge("gy"), y0)
        fill(high_edge("gy"), y1)
        fill(low_edge("gz"), z0)
        fill(high_edge("gz"), z1)

    loads[0].wait()
    loads[1].wait()

    @pl.loop(0, C)
    def _(c):
        a = pl.ds(pl.multiple_of(c * XY, 8), XY)
        b = pl.ds(pl.multiple_of(c * PT, 8), XY)
        gf[b, :] = gb[a, :].astype(jnp.float32)
        nf[b, :] = nb[a, :].astype(jnp.float32)

    acc = None
    for x in range(X):
        cols = []
        for y in range(Y):
            at = pl.ds(x * Y + y, C, stride=PT)
            cols.append(jnp.concatenate([gf[at, :], nf[at, :]], 0).astype(jnp.bfloat16))
        lhs = jnp.concatenate(cols, 1)
        eig_loads[x].wait()
        term = jnp.dot(lhs, eig_v[x], preferred_element_type=jnp.float32)
        acc = term if acc is None else acc + term
    ev = ev_ref[...]
    damp = ev / (ev + 1.0)
    root_damp = 1.0 - 1.0 / jnp.sqrt(1.0 + ev)
    comb = (0.5 * damp) * acc[:C] - root_damp * acc[C:]
    RT = R // 128
    tiles = [(c, r) for c in range(C // 8) for r in range(RT)]
    for t, (c, r) in enumerate(tiles):
        tile = comb[c * 8 : (c + 1) * 8, r * 128 : (r + 1) * 128]
        if rows >= 8:
            o = (t * 8) % rows
            part[(t * 8) // rows, o : o + 8, :] = tile
        else:
            for j in range(8 // rows):
                part[(t * 8) // rows + j] = tile[j * rows : (j + 1) * rows]

    pl.semaphore_wait(barrier, PL - 1 + NZ - 1)

    copies1 = []
    for d in range(1, PL):
        dev, q = plane_peer(d)
        copies1.append(pltpu.make_async_remote_copy(
            src_ref=part.at[q], dst_ref=got1.at[d],
            send_sem=send1.at[d], recv_sem=recv1.at[d],
            device_id=dev, device_id_type=MESH))
    for c in copies1:
        c.start()

    fills()
    loads[2].wait()
    rdv[...] = 1.0 / (rdv[...] + 6.0)

    @pl.loop(0, X)
    def _(x):
        for y in range(Y):
            for g in range(G):
                at = pl.ds(g * CG * PT + x * Y + y, CG, stride=PT)
                src[g, x, y] = -0.5 * gf[at, :] + nf[at, :]

    total = part[me_p]
    for d in range(1, PL):
        copies1[d - 1].wait_recv()
        total = total + got1[d]
    got2[me_z] = total
    copies2 = []
    for d in range(1, NZ):
        copies2.append(pltpu.make_async_remote_copy(
            src_ref=got2.at[me_z], dst_ref=got2.at[me_z],
            send_sem=send2.at[d], recv_sem=recv2.at[d],
            device_id={"gz": lax.rem(me_z + d, NZ)}, device_id_type=MESH))
    for c in copies2:
        c.start()
    for c in copies2:
        c.wait_recv()
    total = got2[0]
    for j in range(1, NZ):
        total = total + got2[j]
    full[me_p] = total
    copies3 = []
    for d in range(1, PL):
        copies3.append(pltpu.make_async_remote_copy(
            src_ref=full.at[me_p], dst_ref=full.at[me_p],
            send_sem=send3.at[d], recv_sem=recv3.at[d],
            device_id=plane_peer(d)[0], device_id_type=MESH))
    for c in copies3:
        c.start()
    for c in copies3:
        c.wait_recv()
    bands = []
    for c in range(C // 8):
        band = []
        for r in range(RT):
            t = c * RT + r
            if rows >= 8:
                o = (t * 8) % rows
                band.append(full[(t * 8) // rows, o : o + 8, :])
            else:
                band.append(jnp.concatenate(
                    [full[(t * 8) // rows + j] for j in range(8 // rows)], 0))
        bands.append(jnp.concatenate(band, 1))
    coef = jnp.concatenate(bands, 0).astype(jnp.bfloat16)

    lane = lax.broadcasted_iota(jnp.int32, (CG, Z), 1)
    pair = lane // 2
    odd = lax.rem(lane, 2) == 1
    at_low = lane == 0
    at_high = lane == Z - 1

    via = count["gx"] == 4

    def relayed(k, g):
        return via and g in RELAYED[k]

    def halo(k, g, axis, sign):
        i = AXES.index(axis) * 2 + (sign > 0)
        n = count[axis]
        recv = hrecv.at[k, g, i]
        to = lax.rem(pos[axis] + (sign + n), n)
        if axis == "gx":
            s = fields.at[k, g, X if sign > 0 else 1, 1 : Y + 1]
            d = fields.at[k, g, 0 if sign > 0 else X + 1, 1 : Y + 1]
        elif axis == "gy":
            s = fields.at[k, g, 1 : X + 1, Y if sign > 0 else 1]
            d = fields.at[k, g, 1 : X + 1, 0 if sign > 0 else Y + 1]
        else:
            s = zout.at[k, g]
            d = zin.at[k, g, 0 if sign > 0 else 1]
        copy = pltpu.make_async_remote_copy(
            src_ref=s, dst_ref=d, send_sem=hsend.at[k, g, i], recv_sem=recv,
            device_id={axis: to}, device_id_type=MESH)
        up, down = pos[axis] < n - 1, pos[axis] > 0
        return copy, (up if sign > 0 else down), (down if sign > 0 else up)

    def hop(k, g, sign):
        i = 1 if sign > 0 else 0
        copy = pltpu.make_async_remote_copy(
            src_ref=fields.at[k, g, X if sign > 0 else 1, 1 : Y + 1], dst_ref=relay.at[k, g],
            send_sem=hsend.at[k, g, i], recv_sem=rrecv.at[k, g],
            device_id={"gx": 3 if sign > 0 else 0}, device_id_type=MESH)
        return copy

    def forward(k, g, sign):
        i = 1 if sign > 0 else 0
        copy = pltpu.make_async_remote_copy(
            src_ref=relay.at[k, g],
            dst_ref=fields.at[k, g, 0 if sign > 0 else X + 1, 1 : Y + 1],
            send_sem=rsend.at[k, g], recv_sem=hrecv.at[k, g, i],
            device_id={"gx": 2 if sign > 0 else 1}, device_id_type=MESH)
        return copy

    ways = [(a, s) for a in AXES if count[a] > 1 for s in (-1, 1)]

    def inner(sign):
        return pos["gx"] == (1 if sign > 0 else 2)

    def send(k, g, axes):
        for a, s in ways:
            if a in axes:
                copy, out, _ = halo(k, g, a, s)
                if a == "gx" and relayed(k, g):
                    pl.when(inner(s))(hop(k, g, s).start)
                    out = out & jnp.logical_not(inner(s))
                pl.when(out)(copy.start)

    def wait_halos(k, g, axes):
        for a, s in ways:
            if a in axes:
                copy, _, come = halo(k, g, a, s)
                pl.when(come)(copy.wait_recv)

    def forwards(k, g, done):
        if relayed(k, g):
            for s, at in ((1, 3), (-1, 0)):
                @pl.when(pos["gx"] == at)
                def _(s=s):
                    if done:
                        forward(k, g, s).wait_send()
                    else:
                        hop(k, g, s).wait_recv()
                        forward(k, g, s).start()

    def wait_sends(k, g):
        for a, s in ways:
            copy, out, _ = halo(k, g, a, s)
            pl.when(out)(copy.wait_send)
        forwards(k, g, True)

    def pack(l, f, old):
        return jnp.where(pair == l, pltpu.roll(f, (2 * l + 1) % Z, 1), old)

    packed = [jnp.zeros((CG, Z), jnp.float32) for _ in range(G)]

    def first(x):
        corr = lax.dot_general(
            coef, eig_v[x], (((1,), (1,)), ((), ())), preferred_element_type=jnp.float32)
        for g in range(G):
            for y in range(Y):
                s = src[g, x, y] + corr[g * CG : (g + 1) * CG, y * Z : (y + 1) * Z]
                src[g, x, y] = s
                f = s * rdv[x, y : y + 1]
                fields[0, g, x + 1, y + 1] = f
                packed[g] = pack(x * Y + y, f, packed[g])

    edges = (0, X - 1) if X > 1 else (0,)
    for x in edges:
        first(x)
    for g in range(G):
        send(0, g, ("gx",))
    for x in range(1, X - 1):
        first(x)
    for g in range(G):
        zout[0, g] = packed[g]
        send(0, g, ("gz", "gy"))

    def step(k, g, x, comb, old):
        for y in range(Y):
            l = x * Y + y
            f = fields[k, g, x + 1, y + 1]
            t = fields[k, g, x + 2, y + 1] + fields[k, g, x, y + 1]
            t = t + (fields[k, g, x + 1, y + 2] + fields[k, g, x + 1, y])
            out = pltpu.roll(comb, (2 * Z - 2 * l - 2) % Z, 1)
            up = jnp.where(at_high, out, pltpu.roll(f, Z - 1, 1))
            down = jnp.where(at_low, out, pltpu.roll(f, 1, 1))
            v = (src[g, x, y] + (t + (up + down))) * rdv[x, y : y + 1]
            if k < S - 1:
                fields[k + 1, g, x + 1, y + 1] = v
                old = pack(l, v, old)
            else:
                at = pl.ds(g * CG * PT + l, CG, stride=PT)
                out_v[at, :] = v + cur_v[at, :]
        return old

    pltpu.make_async_copy(cur_h, cur_v.at[pl.ds(0, C * XY)], load_sem.at[3]).wait()
    zero = jnp.zeros((CG, Z), jnp.float32)
    for k in range(S):
        held, done = {}, []

        def begin(g, k=k, held=held):
            if g not in held:
                wait_halos(k, g, ("gy", "gz"))
                comb = jnp.where(odd, zin[k, g, 1], pltpu.roll(zin[k, g, 0], 2, 1))
                held[g] = [comb, zero]

        for op, g in ((o[0], int(o[1:])) for o in ORDER[k]):
            if op == "F":
                forwards(k, g, False)
                continue
            begin(g)
            if op == "E":
                wait_halos(k, g, ("gx",))
            for x in edges if op == "E" else range(1, X - 1):
                held[g][1] = step(k, g, x, held[g][0], held[g][1])
            done.append(g)
            if k < S - 1:
                if op == "E":
                    send(k + 1, g, ("gx",))
                if done.count(g) == 2:
                    zout[k + 1, g] = held[g][1]
                    send(k + 1, g, ("gy", "gz"))
    for c in copies1 + copies2 + copies3:
        c.wait_send()
    for k in range(S):
        for g in range(G):
            wait_sends(k, g)


def finish(v, out_h, sem):
    C, XY, _ = out_h.shape
    c = pltpu.make_async_copy(v.at[:, pl.ds(0, XY)], out_h, sem)
    c.start()
    c.wait()


def body(sizes, gradient, noise_draw, current, eigvectors, eigvalues, reaction):
    C, X, Y, Z = gradient.shape
    R = eigvectors.shape[3]
    NX, NY, NZ = sizes
    PL = NX * NY
    G = GROUPS
    CG = C // G
    S = SWEEPS - 1
    XY = X * Y
    PT = pitch_of(XY)
    f32, bf16 = jnp.float32, jnp.bfloat16
    rows = C * R // 128 // PL
    any_space = pl.BlockSpec(memory_space=pltpu.HBM)
    vmem = pl.BlockSpec(memory_space=pltpu.VMEM)
    dma = pltpu.SemaphoreType.DMA
    held = pl.pallas_call(
        functools.partial(kernel, sizes, (C, X, Y, Z, R)),
        out_shape=pltpu.VMEM((C * PT, Z), f32),
        in_specs=[any_space] * 4 + [vmem, any_space],
        out_specs=vmem,
        scratch_shapes=[
            pltpu.VMEM((X, Y * Z, R), bf16),
            pltpu.VMEM((C * XY, Z), bf16),
            pltpu.VMEM((C * XY, Z), bf16),
            pltpu.VMEM((C * PT, Z), f32),
            pltpu.VMEM((C * PT, Z), f32),
            pltpu.VMEM((C * PT, Z), f32),
            pltpu.VMEM((X, Y, Z), f32),
            pltpu.VMEM((G, X, Y, CG, Z), f32),
            pltpu.VMEM((S, G, X + 2, Y + 2, CG, Z), f32),
            pltpu.VMEM((S, G, CG, Z), f32),
            pltpu.VMEM((S, G, 2, CG, Z), f32),
            pltpu.VMEM((S, G, Y, CG, Z), f32),
            pltpu.VMEM((PL, rows, 128), f32),
            pltpu.VMEM((PL, rows, 128), f32),
            pltpu.VMEM((NZ, rows, 128), f32),
            pltpu.VMEM((PL, rows, 128), f32),
            dma((4 + X,)),
            dma((PL,)), dma((PL,)),
            dma((NZ,)), dma((NZ,)),
            dma((PL,)), dma((PL,)),
            dma((S, G, 6)), dma((S, G, 6)),
            dma((S, G)), dma((S, G)),
        ],
        compiler_params=pltpu.CompilerParams(
            collective_id=0, has_side_effects=True, vmem_limit_bytes=67043328 - C * PT * Z * 4 - LEFT
        ),
    )(
        gradient.reshape(C * XY, Z),
        noise_draw.reshape(C * XY, Z),
        current.reshape(C * XY, Z),
        eigvectors.reshape(X, Y * Z, R),
        eigvalues.reshape(1, R),
        reaction,
    )
    out = pl.pallas_call(
        finish,
        out_shape=jax.ShapeDtypeStruct((C, XY, Z), f32),
        in_specs=[vmem],
        out_specs=any_space,
        scratch_shapes=[dma],
        compiler_params=pltpu.CompilerParams(vmem_limit_bytes=4 * 1024 * 1024),
    )(held.reshape(C, PT, Z))
    return out.reshape(current.shape)


def solution(mesh):
    return jax.shard_map(
        functools.partial(body, tuple(mesh.shape[a] for a in AXES)),
        mesh=mesh,
        in_specs=(
            P(None, "gx", "gy", "gz"),
            P(None, "gx", "gy", "gz"),
            P(None, "gx", "gy", "gz"),
            P("gx", "gy", "gz", None),
            P(),
            P("gx", "gy", "gz"),
        ),
        out_specs=P(None, "gx", "gy", "gz"),
        check_vma=False,
    )
```

time: 44.9 us -> 40 us (0.89)
  Pallas kernels: 42.4 us -> 39.8 us
  local copies, waits for them, and re-layouts: 2.31 us -> 0 us
    pallas_call x1, Pallas kernels: 42.4 us -> 38.8 us  [body(): pl.pallas_call(functools.partial(kernel, sizes, (C, X, Y, Z, R)), out_sha...]
    unnamed x1 -> x0, local copies, waits for them, and re-layouts: 2.31 us -> none
    pallas_call x0 -> x1, Pallas kernels: none -> 0.98 us  [body(): pl.pallas_call(finish, out_shape=jax.ShapeDtypeStruct((C, XY, Z), f32), i...]
where the time goes in v1:
time: 40 us; the launch traced here: 39.8 us
  Pallas kernels  39.8 us (99%)
    pallas_call x1, Pallas kernels, body(): pl.pallas_call(functools.partial(kernel, sizes, (C, X, Y, Z, R)), out_sha...  38.8 us
    pallas_call x1, Pallas kernels, body(): pl.pallas_call(finish, out_shape=jax.ShapeDtypeStruct((C, XY, Z), f32), i...  0.98 us

profile of v1, /device:TPU:0, one launch (start us, length us, event | category | flops | bytes accessed | tf_op | source)
XLA Modules:
  0.0 39.8 jit_solution(12991441702980609038)
XLA Ops:
  0.0 38.8 %shard_map.64 = f32[2304,128]{1,0:T(8,128)S(1)} custom-call(bf16[2048,128]{1,0:T(8,128)(2,1)} %bitcast.10, bf16[2048,128]{1,0:T(8,128)(2,1)} %bitcast.11, f32[2048,128]{1,0:T(8,128)} %bitcast.9, bf16[8,1024,512]{2,1,0:T(8,128)(2,1)} %bitcast.8, f32[1,512]{1,0:T(1,128)} %bitcast.12, f32[8,8,128]{2,1,0:T(8,128)} %rea_h.1), custom_call_target="tpu_custom_call" | custom-call | tf_op jit(solution)/shard_map/pallas_call | solution.py:411
  38.8 1.0 %shard_map.65 = f32[32,64,128]{2,1,0:T(8,128)} custom-call(f32[32,72,128]{2,1,0:T(8,128)S(1)} %bitcast.7), custom_call_target="tpu_custom_call" | custom-call | tf_op jit(solution)/shard_map/pallas_call | solution.py:451

commit v2 on v1

--- a/solution.py
+++ b/solution.py
@@ -9,13 +9,10 @@
 
 SWEEPS = 4
 GROUPS = 4
+HALVES = 2
 LEFT = 65536
-RELAYED = ((2, 3), (2, 3), ())
-ORDER = (
-    ("F2", "F3", "E0", "E1", "I0", "I1", "E2", "I2", "E3", "I3"),
-    ("F2", "F3", "I0", "E0", "I1", "E1", "I2", "E2", "I3", "E3"),
-    ("F2", "F3", "I0", "E0", "I1", "E1", "I2", "E2", "I3", "E3"),
-)
+RELAYED = ((2, 3), (3,), ())
+ORDER = (("F2", "F3", "E0", "E1", "I0", "I1", "E2", "I2", "E3", "I3"), ("F3", "I0", "E0", "I1", "E1", "I2", "E2", "I3", "E3"), ("F2", "F3", "I0", "E0", "I1", "E1", "I2", "E2", "I3", "E3"))
 MESH = pl.DeviceIdType.MESH
 AXES = ("gx", "gy", "gz")
 
@@ -25,10 +22,10 @@
 
 
 def kernel(
-    sizes, shape, g_h, n_h, cur_h, eig_h, ev_ref, rea_h, out_v,
-    eig_v, gb, nb, gf, nf, cur_v, rdv, src, fields, zout, zin, relay,
+    sizes, shape, g_h, n_h, cur_h, eig_h, ev_h, rea_h, out_v,
+    eig_v, gb, nb, gf, nf, cur_v, ev_v, rdv, src, fields, zout, zin, relay,
     part, got1, got2, full, load_sem,
-    send1, recv1, send2, recv2, send3, recv3, hsend, hrecv, rsend, rrecv,
+    send_sem, recv1, recv2, recv3, hsend, xrecv, yzrecv, rsend, rrecv,
 ):
     C, X, Y, Z, R = shape
     NX, NY, NZ = sizes
@@ -48,18 +45,13 @@
         pltpu.make_async_copy(g_h, gb, load_sem.at[0]),
         pltpu.make_async_copy(n_h, nb, load_sem.at[1]),
         pltpu.make_async_copy(rea_h, rdv, load_sem.at[2]),
+        pltpu.make_async_copy(ev_h, ev_v, load_sem.at[4]),
     ]
     eig_loads = [
-        pltpu.make_async_copy(eig_h.at[x], eig_v.at[x], load_sem.at[4 + x]) for x in range(X)
+        pltpu.make_async_copy(eig_h.at[x], eig_v.at[x], load_sem.at[5 + x]) for x in range(X)
     ]
-    for c in loads + eig_loads:
+    for c in loads[:2] + eig_loads + loads[2:]:
         c.start()
-
-    @pl.loop(0, C)
-    def _(c):
-        a = pl.ds(pl.multiple_of(c * XY, 8), XY)
-        b = pl.ds(pl.multiple_of(c * PT, 8), XY)
-        pltpu.make_async_copy(cur_h.at[a], cur_v.at[b], load_sem.at[3]).start()
 
     barrier = pltpu.get_barrier_semaphore()
 
@@ -141,7 +133,8 @@
         eig_loads[x].wait()
         term = jnp.dot(lhs, eig_v[x], preferred_element_type=jnp.float32)
         acc = term if acc is None else acc + term
-    ev = ev_ref[...]
+    loads[3].wait()
+    ev = ev_v[...]
     damp = ev / (ev + 1.0)
     root_damp = 1.0 - 1.0 / jnp.sqrt(1.0 + ev)
     comb = (0.5 * damp) * acc[:C] - root_damp * acc[C:]
@@ -163,10 +156,16 @@
         dev, q = plane_peer(d)
         copies1.append(pltpu.make_async_remote_copy(
             src_ref=part.at[q], dst_ref=got1.at[d],
-            send_sem=send1.at[d], recv_sem=recv1.at[d],
+            send_sem=send_sem.at[0], recv_sem=recv1.at[d - 1],
             device_id=dev, device_id_type=MESH))
     for c in copies1:
         c.start()
+
+    @pl.loop(0, C)
+    def _(c):
+        a = pl.ds(pl.multiple_of(c * XY, 8), XY)
+        b = pl.ds(pl.multiple_of(c * PT, 8), XY)
+        pltpu.make_async_copy(cur_h.at[a], cur_v.at[b], load_sem.at[3]).start()
 
     fills()
     loads[2].wait()
@@ -188,7 +187,7 @@
     for d in range(1, NZ):
         copies2.append(pltpu.make_async_remote_copy(
             src_ref=got2.at[me_z], dst_ref=got2.at[me_z],
-            send_sem=send2.at[d], recv_sem=recv2.at[d],
+            send_sem=send_sem.at[1], recv_sem=recv2.at[d - 1],
             device_id={"gz": lax.rem(me_z + d, NZ)}, device_id_type=MESH))
     for c in copies2:
         c.start()
@@ -202,7 +201,7 @@
     for d in range(1, PL):
         copies3.append(pltpu.make_async_remote_copy(
             src_ref=full.at[me_p], dst_ref=full.at[me_p],
-            send_sem=send3.at[d], recv_sem=recv3.at[d],
+            send_sem=send_sem.at[2], recv_sem=recv3.at[d - 1],
             device_id=plane_peer(d)[0], device_id_type=MESH))
     for c in copies3:
         c.start()
@@ -224,19 +223,24 @@
 
     lane = lax.broadcasted_iota(jnp.int32, (CG, Z), 1)
     pair = lane // 2
+    zero = jnp.zeros((CG, Z), jnp.float32)
     odd = lax.rem(lane, 2) == 1
     at_low = lane == 0
     at_high = lane == Z - 1
 
     via = count["gx"] == 4
 
+    relays = [(k, g) for k in range(S) for g in RELAYED[k]] if via else []
+    H = yzrecv.shape[1]
+    GH = G // H
+
     def relayed(k, g):
-        return via and g in RELAYED[k]
+        return (k, g) in relays
 
     def halo(k, g, axis, sign):
         i = AXES.index(axis) * 2 + (sign > 0)
         n = count[axis]
-        recv = hrecv.at[k, g, i]
+        recv = xrecv.at[k, g, i] if axis == "gx" else yzrecv.at[k, g // GH, i - 2]
         to = lax.rem(pos[axis] + (sign + n), n)
         if axis == "gx":
             s = fields.at[k, g, X if sign > 0 else 1, 1 : Y + 1]
@@ -248,7 +252,7 @@
             s = zout.at[k, g]
             d = zin.at[k, g, 0 if sign > 0 else 1]
         copy = pltpu.make_async_remote_copy(
-            src_ref=s, dst_ref=d, send_sem=hsend.at[k, g, i], recv_sem=recv,
+            src_ref=s, dst_ref=d, send_sem=hsend.at[i], recv_sem=recv,
             device_id={axis: to}, device_id_type=MESH)
         up, down = pos[axis] < n - 1, pos[axis] > 0
         return copy, (up if sign > 0 else down), (down if sign > 0 else up)
@@ -256,17 +260,18 @@
     def hop(k, g, sign):
         i = 1 if sign > 0 else 0
         copy = pltpu.make_async_remote_copy(
-            src_ref=fields.at[k, g, X if sign > 0 else 1, 1 : Y + 1], dst_ref=relay.at[k, g],
-            send_sem=hsend.at[k, g, i], recv_sem=rrecv.at[k, g],
+            src_ref=fields.at[k, g, X if sign > 0 else 1, 1 : Y + 1],
+            dst_ref=relay.at[relays.index((k, g))],
+            send_sem=hsend.at[i], recv_sem=rrecv.at[relays.index((k, g))],
             device_id={"gx": 3 if sign > 0 else 0}, device_id_type=MESH)
         return copy
 
     def forward(k, g, sign):
         i = 1 if sign > 0 else 0
         copy = pltpu.make_async_remote_copy(
-            src_ref=relay.at[k, g],
+            src_ref=relay.at[relays.index((k, g))],
             dst_ref=fields.at[k, g, 0 if sign > 0 else X + 1, 1 : Y + 1],
-            send_sem=rsend.at[k, g], recv_sem=hrecv.at[k, g, i],
+            send_sem=rsend.at[0], recv_sem=xrecv.at[k, g, i],
             device_id={"gx": 2 if sign > 0 else 1}, device_id_type=MESH)
         return copy
 
@@ -275,42 +280,72 @@
     def inner(sign):
         return pos["gx"] == (1 if sign > 0 else 2)
 
-    def send(k, g, axes):
+    def send(k, g, axes, signs=(-1, 1)):
+        go = []
         for a, s in ways:
-            if a in axes:
+            if a in axes and s in signs:
                 copy, out, _ = halo(k, g, a, s)
-                if a == "gx" and relayed(k, g):
-                    pl.when(inner(s))(hop(k, g, s).start)
+                if a == "gx" and via:
+                    go.insert(0, (inner(s), hop(k, g, s) if relayed(k, g) else copy))
                     out = out & jnp.logical_not(inner(s))
-                pl.when(out)(copy.start)
-
-    def wait_halos(k, g, axes):
+                go.append((out, copy))
+        for out, copy in go:
+            pl.when(out)(copy.start)
+
+    def wait_x(k, g):
         for a, s in ways:
-            if a in axes:
+            if a == "gx":
                 copy, _, come = halo(k, g, a, s)
                 pl.when(come)(copy.wait_recv)
 
-    def forwards(k, g, done):
+    def wait_yz(k, h):
+        r = pl.ds(h * GH, GH)
+        for a, s in ways:
+            if a == "gx":
+                continue
+            i = AXES.index(a) * 2 + (s > 0)
+            if a == "gy":
+                d = fields.at[k, r, 1 : X + 1, 0 if s > 0 else Y + 1]
+            else:
+                d = zin.at[k, r, 0 if s > 0 else 1]
+            come = pos[a] > 0 if s > 0 else pos[a] < count[a] - 1
+            pl.when(come)(pltpu.make_async_copy(d, d, yzrecv.at[k, h, i - 2]).wait)
+
+    def forwards(k, g):
         if relayed(k, g):
             for s, at in ((1, 3), (-1, 0)):
                 @pl.when(pos["gx"] == at)
                 def _(s=s):
-                    if done:
-                        forward(k, g, s).wait_send()
-                    else:
-                        hop(k, g, s).wait_recv()
-                        forward(k, g, s).start()
-
-    def wait_sends(k, g):
+                    hop(k, g, s).wait_recv()
+                    forward(k, g, s).start()
+
+    def wait_sends():
         for a, s in ways:
-            copy, out, _ = halo(k, g, a, s)
-            pl.when(out)(copy.wait_send)
-        forwards(k, g, True)
-
-    def pack(l, f, old):
-        return jnp.where(pair == l, pltpu.roll(f, (2 * l + 1) % Z, 1), old)
-
-    packed = [jnp.zeros((CG, Z), jnp.float32) for _ in range(G)]
+            i = AXES.index(a) * 2 + (s > 0)
+            if a == "gx":
+                d = fields.at[:, :, X if s > 0 else 1, 1 : Y + 1]
+            elif a == "gy":
+                d = fields.at[:, :, 1 : X + 1, Y if s > 0 else 1]
+            else:
+                d = zout
+            out = pos[a] < count[a] - 1 if s > 0 else pos[a] > 0
+            pl.when(out)(pltpu.make_async_copy(d, d, hsend.at[i]).wait)
+        if relays:
+            @pl.when((pos["gx"] == 0) | (pos["gx"] == 3))
+            def _():
+                pltpu.make_async_copy(relay, relay, rsend.at[0]).wait()
+        for d, i in ((part.at[pl.ds(0, PL - 1)], 0), (got2.at[pl.ds(0, NZ - 1)], 1), (full.at[pl.ds(0, PL - 1)], 2)):
+            if d.shape[0]:
+                pltpu.make_async_copy(d, d, send_sem.at[i]).wait()
+
+    def pack(k, g):
+        out = zero
+        for x in range(X):
+            for y in range(Y):
+                l = x * Y + y
+                f = pltpu.roll(fields[k, g, x + 1, y + 1], (2 * l + 1) % Z, 1)
+                out = jnp.where(pair == l, f, out)
+        zout[k, g] = out
 
     def first(x):
         corr = lax.dot_general(
@@ -321,20 +356,21 @@
                 src[g, x, y] = s
                 f = s * rdv[x, y : y + 1]
                 fields[0, g, x + 1, y + 1] = f
-                packed[g] = pack(x * Y + y, f, packed[g])
 
     edges = (0, X - 1) if X > 1 else (0,)
     for x in edges:
         first(x)
-    for g in range(G):
-        send(0, g, ("gx",))
+        for g in range(G):
+            send(0, g, ("gx",), (-1 if x == 0 else 1,) if X > 1 else (-1, 1))
     for x in range(1, X - 1):
         first(x)
     for g in range(G):
-        zout[0, g] = packed[g]
-        send(0, g, ("gz", "gy"))
-
-    def step(k, g, x, comb, old):
+        send(0, g, ("gy",))
+    for g in range(G):
+        pack(0, g)
+        send(0, g, ("gz",))
+
+    def step(k, g, x, comb):
         for y in range(Y):
             l = x * Y + y
             f = fields[k, g, x + 1, y + 1]
@@ -346,44 +382,40 @@
             v = (src[g, x, y] + (t + (up + down))) * rdv[x, y : y + 1]
             if k < S - 1:
                 fields[k + 1, g, x + 1, y + 1] = v
-                old = pack(l, v, old)
             else:
                 at = pl.ds(g * CG * PT + l, CG, stride=PT)
                 out_v[at, :] = v + cur_v[at, :]
-        return old
 
     pltpu.make_async_copy(cur_h, cur_v.at[pl.ds(0, C * XY)], load_sem.at[3]).wait()
-    zero = jnp.zeros((CG, Z), jnp.float32)
     for k in range(S):
-        held, done = {}, []
-
-        def begin(g, k=k, held=held):
+        held, done, ready = {}, [], []
+
+        def begin(g, k=k, held=held, ready=ready):
             if g not in held:
-                wait_halos(k, g, ("gy", "gz"))
+                if g // GH not in ready:
+                    ready.append(g // GH)
+                    wait_yz(k, g // GH)
                 comb = jnp.where(odd, zin[k, g, 1], pltpu.roll(zin[k, g, 0], 2, 1))
-                held[g] = [comb, zero]
+                held[g] = comb
 
         for op, g in ((o[0], int(o[1:])) for o in ORDER[k]):
             if op == "F":
-                forwards(k, g, False)
+                forwards(k, g)
                 continue
             begin(g)
             if op == "E":
-                wait_halos(k, g, ("gx",))
+                wait_x(k, g)
             for x in edges if op == "E" else range(1, X - 1):
-                held[g][1] = step(k, g, x, held[g][0], held[g][1])
+                step(k, g, x, held[g])
             done.append(g)
             if k < S - 1:
                 if op == "E":
                     send(k + 1, g, ("gx",))
                 if done.count(g) == 2:
-                    zout[k + 1, g] = held[g][1]
-                    send(k + 1, g, ("gy", "gz"))
-    for c in copies1 + copies2 + copies3:
-        c.wait_send()
-    for k in range(S):
-        for g in range(G):
-            wait_sends(k, g)
+                    send(k + 1, g, ("gy",))
+                    pack(k + 1, g)
+                    send(k + 1, g, ("gz",))
+    wait_sends()
 
 
 def finish(v, out_h, sem):
@@ -405,13 +437,14 @@
     PT = pitch_of(XY)
     f32, bf16 = jnp.float32, jnp.bfloat16
     rows = C * R // 128 // PL
+    NR = max(sum(len(r) for r in RELAYED), 1)
     any_space = pl.BlockSpec(memory_space=pltpu.HBM)
     vmem = pl.BlockSpec(memory_space=pltpu.VMEM)
     dma = pltpu.SemaphoreType.DMA
     held = pl.pallas_call(
         functools.partial(kernel, sizes, (C, X, Y, Z, R)),
         out_shape=pltpu.VMEM((C * PT, Z), f32),
-        in_specs=[any_space] * 4 + [vmem, any_space],
+        in_specs=[any_space] * 6,
         out_specs=vmem,
         scratch_shapes=[
             pltpu.VMEM((X, Y * Z, R), bf16),
@@ -420,22 +453,22 @@
             pltpu.VMEM((C * PT, Z), f32),
             pltpu.VMEM((C * PT, Z), f32),
             pltpu.VMEM((C * PT, Z), f32),
+            pltpu.VMEM((1, R), f32),
             pltpu.VMEM((X, Y, Z), f32),
             pltpu.VMEM((G, X, Y, CG, Z), f32),
             pltpu.VMEM((S, G, X + 2, Y + 2, CG, Z), f32),
             pltpu.VMEM((S, G, CG, Z), f32),
             pltpu.VMEM((S, G, 2, CG, Z), f32),
-            pltpu.VMEM((S, G, Y, CG, Z), f32),
+            pltpu.VMEM((NR, Y, CG, Z), f32),
             pltpu.VMEM((PL, rows, 128), f32),
             pltpu.VMEM((PL, rows, 128), f32),
             pltpu.VMEM((NZ, rows, 128), f32),
             pltpu.VMEM((PL, rows, 128), f32),
-            dma((4 + X,)),
-            dma((PL,)), dma((PL,)),
-            dma((NZ,)), dma((NZ,)),
-            dma((PL,)), dma((PL,)),
-            dma((S, G, 6)), dma((S, G, 6)),
-            dma((S, G)), dma((S, G)),
+            dma((5 + X,)),
+            dma((3,)),
+            dma((max(PL - 1, 1),)), dma((max(NZ - 1, 1),)), dma((max(PL - 1, 1),)),
+            dma((6,)), dma((S, G, 2)), dma((S, HALVES, 4)),
+            dma((1,)), dma((NR,)),
         ],
         compiler_params=pltpu.CompilerParams(
             collective_id=0, has_side_effects=True, vmem_limit_bytes=67043328 - C * PT * Z * 4 - LEFT

time: 40 us -> 38 us (0.950)
  Pallas kernels: 39.8 us -> 37.8 us
    pallas_call x1, Pallas kernels: 38.8 us -> 36.8 us  [body(): pl.pallas_call(functools.partial(kernel, sizes, (C, X, Y, Z, R)), out_sha...]
where the time goes in v2:
time: 38 us; the launch traced here: 37.8 us
  Pallas kernels  37.8 us (99%)
    pallas_call x1, Pallas kernels, body(): pl.pallas_call(functools.partial(kernel, sizes, (C, X, Y, Z, R)), out_sha...  36.8 us
    pallas_call x1, Pallas kernels, body(): pl.pallas_call(finish, out_shape=jax.ShapeDtypeStruct((C, XY, Z), f32), i...  0.98 us

profile of v2, /device:TPU:0, one launch (start us, length us, event | category | flops | bytes accessed | tf_op | source)
XLA Modules:
  0.0 37.8 jit_solution(13107439603823685553)
XLA Ops:
  0.0 36.8 %shard_map.64 = f32[2304,128]{1,0:T(8,128)S(1)} custom-call(bf16[2048,128]{1,0:T(8,128)(2,1)} %bitcast.10, bf16[2048,128]{1,0:T(8,128)(2,1)} %bitcast.11, f32[2048,128]{1,0:T(8,128)} %bitcast.9, bf16[8,1024,512]{2,1,0:T(8,128)(2,1)} %bitcast.8, f32[1,512]{1,0:T(1,128)} %bitcast.12, f32[8,8,128]{2,1,0:T(8,128)} %rea_h.1), custom_call_target="tpu_custom_call" | custom-call | tf_op jit(solution)/shard_map/pallas_call | solution.py:444
  36.8 1.0 %shard_map.65 = f32[32,64,128]{2,1,0:T(8,128)} custom-call(f32[32,72,128]{2,1,0:T(8,128)S(1)} %bitcast.7), custom_call_target="tpu_custom_call" | custom-call | tf_op jit(solution)/shard_map/pallas_call | solution.py:484

commit v3 on v2

--- a/solution.py
+++ b/solution.py
@@ -10,9 +10,10 @@
 SWEEPS = 4
 GROUPS = 4
 HALVES = 2
+FLIGHT = 8
 LEFT = 65536
-RELAYED = ((2, 3), (3,), ())
-ORDER = (("F2", "F3", "E0", "E1", "I0", "I1", "E2", "I2", "E3", "I3"), ("F3", "I0", "E0", "I1", "E1", "I2", "E2", "I3", "E3"), ("F2", "F3", "I0", "E0", "I1", "E1", "I2", "E2", "I3", "E3"))
+RELAYED = ((2, 3), (0,), (0,))
+ORDER = (("F2", "F3", "E0", "E1", "I0", "I1", "E2", "E3", "I2", "I3"), ("F0", "I0", "E0", "I1", "E1", "I2", "E2", "I3", "E3"), ("F0", "I0", "E0", "I1", "E1", "I2", "E2", "I3", "E3"))
 MESH = pl.DeviceIdType.MESH
 AXES = ("gx", "gy", "gz")
 
@@ -23,9 +24,9 @@
 
 def kernel(
     sizes, shape, g_h, n_h, cur_h, eig_h, ev_h, rea_h, out_v,
-    eig_v, gb, nb, gf, nf, cur_v, ev_v, rdv, src, fields, zout, zin, relay,
+    eig_v, gb, nb, gf, nf, cur_v, ev_v, rdv, src, fields, zout, zin, zout_e, zin_e, relay,
     part, got1, got2, full, load_sem,
-    send_sem, recv1, recv2, recv3, hsend, xrecv, yzrecv, rsend, rrecv,
+    send_sem, recv1, recv2, recv3, hsend, xrecv, yzrecv, early, rsend, rrecv,
 ):
     C, X, Y, Z, R = shape
     NX, NY, NZ = sizes
@@ -39,6 +40,14 @@
     pos = {a: lax.axis_index(a) for a in AXES}
     count = dict(zip(AXES, sizes))
     me_p = pos["gx"] * NY + pos["gy"]
+    OW = 2 if NY % 2 == 0 else 1
+    NO = PL // OW
+
+    def owns(q):
+        return True if OW == 1 else lax.rem(q, OW) == OW - 1
+
+    mine = owns(me_p)
+    me_o = me_p // OW
     me_z = pos["gz"]
 
     loads = [
@@ -50,7 +59,7 @@
     eig_loads = [
         pltpu.make_async_copy(eig_h.at[x], eig_v.at[x], load_sem.at[5 + x]) for x in range(X)
     ]
-    for c in loads[:2] + eig_loads + loads[2:]:
+    for c in loads[:2] + eig_loads[:FLIGHT]:
         c.start()
 
     barrier = pltpu.get_barrier_semaphore()
@@ -74,6 +83,8 @@
             fn()
         else:
             pl.when(cond)(fn)
+
+    when = fill
 
     def low_edge(a):
         return True if count[a] == 1 else pos[a] == 0
@@ -102,10 +113,12 @@
             for k in range(S):
                 for g in range(G):
                     zin[k, g, 0] = jnp.zeros((CG, Z), jnp.float32)
+            zin_e[0] = jnp.zeros((G, CG, Z), jnp.float32)
         def z1():
             for k in range(S):
                 for g in range(G):
                     zin[k, g, 1] = jnp.zeros((CG, Z), jnp.float32)
+            zin_e[1] = jnp.zeros((G, CG, Z), jnp.float32)
         fill(low_edge("gx"), x0)
         fill(high_edge("gx"), x1)
         fill(low_edge("gy"), y0)
@@ -131,6 +144,8 @@
             cols.append(jnp.concatenate([gf[at, :], nf[at, :]], 0).astype(jnp.bfloat16))
         lhs = jnp.concatenate(cols, 1)
         eig_loads[x].wait()
+        for c in eig_loads[x + FLIGHT : x + FLIGHT + 1] or (loads[2:] if x == max(X - FLIGHT, 0) else []):
+            c.start()
         term = jnp.dot(lhs, eig_v[x], preferred_element_type=jnp.float32)
         acc = term if acc is None else acc + term
     loads[3].wait()
@@ -155,11 +170,10 @@
     for d in range(1, PL):
         dev, q = plane_peer(d)
         copies1.append(pltpu.make_async_remote_copy(
-            src_ref=part.at[q], dst_ref=got1.at[d],
+            src_ref=part.at[q // OW], dst_ref=got1.at[d],
             send_sem=send_sem.at[0], recv_sem=recv1.at[d - 1],
             device_id=dev, device_id_type=MESH))
-    for c in copies1:
-        c.start()
+        when(owns(q), copies1[-1].start)
 
     @pl.loop(0, C)
     def _(c):
@@ -178,35 +192,38 @@
                 at = pl.ds(g * CG * PT + x * Y + y, CG, stride=PT)
                 src[g, x, y] = -0.5 * gf[at, :] + nf[at, :]
 
-    total = part[me_p]
+    def reduce1():
+        total = part[me_o]
+        for d in range(1, PL):
+            copies1[d - 1].wait_recv()
+            total = total + got1[d]
+        got2[me_z] = total
+    when(mine, reduce1)
+    def reduce2():
+        copies = []
+        for d in range(1, NZ):
+            copies.append(pltpu.make_async_remote_copy(
+                src_ref=got2.at[me_z], dst_ref=got2.at[me_z],
+                send_sem=send_sem.at[1], recv_sem=recv2.at[d - 1],
+                device_id={"gz": lax.rem(me_z + d, NZ)}, device_id_type=MESH))
+        for c in copies:
+            c.start()
+        for c in copies:
+            c.wait_recv()
+        total = got2[0]
+        for j in range(1, NZ):
+            total = total + got2[j]
+        full[me_o] = total
+        for d in range(1, PL):
+            pltpu.make_async_remote_copy(
+                src_ref=full.at[me_o], dst_ref=full.at[me_o],
+                send_sem=send_sem.at[2], recv_sem=recv3.at[d - 1],
+                device_id=plane_peer(d)[0], device_id_type=MESH).start()
+    when(mine, reduce2)
     for d in range(1, PL):
-        copies1[d - 1].wait_recv()
-        total = total + got1[d]
-    got2[me_z] = total
-    copies2 = []
-    for d in range(1, NZ):
-        copies2.append(pltpu.make_async_remote_copy(
-            src_ref=got2.at[me_z], dst_ref=got2.at[me_z],
-            send_sem=send_sem.at[1], recv_sem=recv2.at[d - 1],
-            device_id={"gz": lax.rem(me_z + d, NZ)}, device_id_type=MESH))
-    for c in copies2:
-        c.start()
-    for c in copies2:
-        c.wait_recv()
-    total = got2[0]
-    for j in range(1, NZ):
-        total = total + got2[j]
-    full[me_p] = total
-    copies3 = []
-    for d in range(1, PL):
-        copies3.append(pltpu.make_async_remote_copy(
-            src_ref=full.at[me_p], dst_ref=full.at[me_p],
-            send_sem=send_sem.at[2], recv_sem=recv3.at[d - 1],
-            device_id=plane_peer(d)[0], device_id_type=MESH))
-    for c in copies3:
-        c.start()
-    for c in copies3:
-        c.wait_recv()
+        q = lax.rem(me_p + (PL - d), PL)
+        r = full.at[q // OW]
+        when(owns(q), pltpu.make_async_copy(r, r, recv3.at[d - 1]).wait)
     bands = []
     for c in range(C // 8):
         band = []
@@ -234,6 +251,38 @@
     H = yzrecv.shape[1]
     GH = G // H
 
+    inner_rows = slice(2, X)
+
+    def early_copies(axis, sign):
+        n = count[axis]
+        dev = {axis: lax.rem(pos[axis] + (sign + n), n)}
+        i = AXES.index(axis) * 2 + (sign > 0)
+        if axis == "gz":
+            pairs = [(zout_e, zin_e.at[0 if sign > 0 else 1])]
+            i = 6 + (sign > 0)
+        else:
+            pairs = [(fields.at[0, :, x, Y if sign > 0 else 1], fields.at[0, :, x, 0 if sign > 0 else Y + 1])
+                     for x in (1, X)]
+        return [pltpu.make_async_remote_copy(
+            src_ref=a, dst_ref=b, send_sem=hsend.at[i],
+            recv_sem=early.at[AXES.index(axis) * 2 - 2 + (sign > 0)],
+            device_id=dev, device_id_type=MESH) for a, b in pairs]
+
+    def send_early():
+        for a, s in ways:
+            if a != "gx":
+                out = pos[a] < count[a] - 1 if s > 0 else pos[a] > 0
+                for c in early_copies(a, s):
+                    pl.when(out)(c.start)
+
+    def wait_early():
+        for a, s in ways:
+            if a != "gx":
+                come = pos[a] > 0 if s > 0 else pos[a] < count[a] - 1
+                d = zin_e.at[0] if a == "gz" else fields.at[0, :, pl.ds(1, 2), 0]
+                i = AXES.index(a) * 2 - 2 + (s > 0)
+                pl.when(come)(pltpu.make_async_copy(d, d, early.at[i]).wait)
+
     def relayed(k, g):
         return (k, g) in relays
 
@@ -246,8 +295,9 @@
             s = fields.at[k, g, X if sign > 0 else 1, 1 : Y + 1]
             d = fields.at[k, g, 0 if sign > 0 else X + 1, 1 : Y + 1]
         elif axis == "gy":
-            s = fields.at[k, g, 1 : X + 1, Y if sign > 0 else 1]
-            d = fields.at[k, g, 1 : X + 1, 0 if sign > 0 else Y + 1]
+            r = inner_rows if k == 0 else slice(1, X + 1)
+            s = fields.at[k, g, r, Y if sign > 0 else 1]
+            d = fields.at[k, g, r, 0 if sign > 0 else Y + 1]
         else:
             s = zout.at[k, g]
             d = zin.at[k, g, 0 if sign > 0 else 1]
@@ -280,13 +330,16 @@
     def inner(sign):
         return pos["gx"] == (1 if sign > 0 else 2)
 
-    def send(k, g, axes, signs=(-1, 1)):
+    def send(k, g, axes, signs=(-1, 1), also=None):
         go = []
         for a, s in ways:
             if a in axes and s in signs:
                 copy, out, _ = halo(k, g, a, s)
+                if also is not None:
+                    out = out & also
                 if a == "gx" and via:
-                    go.insert(0, (inner(s), hop(k, g, s) if relayed(k, g) else copy))
+                    far = inner(s) if also is None else inner(s) & also
+                    go.insert(0, (far, hop(k, g, s) if relayed(k, g) else copy))
                     out = out & jnp.logical_not(inner(s))
                 go.append((out, copy))
         for out, copy in go:
@@ -305,7 +358,7 @@
                 continue
             i = AXES.index(a) * 2 + (s > 0)
             if a == "gy":
-                d = fields.at[k, r, 1 : X + 1, 0 if s > 0 else Y + 1]
+                d = fields.at[k, r, inner_rows if k == 0 else slice(1, X + 1), 0 if s > 0 else Y + 1]
             else:
                 d = zin.at[k, r, 0 if s > 0 else 1]
             come = pos[a] > 0 if s > 0 else pos[a] < count[a] - 1
@@ -330,13 +383,26 @@
                 d = zout
             out = pos[a] < count[a] - 1 if s > 0 else pos[a] > 0
             pl.when(out)(pltpu.make_async_copy(d, d, hsend.at[i]).wait)
+            if a == "gz":
+                pl.when(out)(pltpu.make_async_copy(zout_e, zout_e, hsend.at[6 + (s > 0)]).wait)
         if relays:
             @pl.when((pos["gx"] == 0) | (pos["gx"] == 3))
             def _():
                 pltpu.make_async_copy(relay, relay, rsend.at[0]).wait()
-        for d, i in ((part.at[pl.ds(0, PL - 1)], 0), (got2.at[pl.ds(0, NZ - 1)], 1), (full.at[pl.ds(0, PL - 1)], 2)):
-            if d.shape[0]:
-                pltpu.make_async_copy(d, d, send_sem.at[i]).wait()
+
+        def sent(i, n, buf):
+            if n:
+                r = buf.at[pl.ds(0, n)]
+                pltpu.make_async_copy(r, r, send_sem.at[i]).wait()
+
+        def owned():
+            sent(0, NO - 1, part)
+            sent(1, NZ - 1, got2)
+            sent(2, PL - 1, got1)
+
+        when(mine, owned)
+        if OW > 1:
+            when(jnp.logical_not(mine), lambda: sent(0, NO, part))
 
     def pack(k, g):
         out = zero
@@ -346,6 +412,15 @@
                 f = pltpu.roll(fields[k, g, x + 1, y + 1], (2 * l + 1) % Z, 1)
                 out = jnp.where(pair == l, f, out)
         zout[k, g] = out
+
+    def pack_edges(g):
+        out = zero
+        for x in (0, X - 1):
+            for y in range(Y):
+                l = x * Y + y
+                f = pltpu.roll(fields[0, g, x + 1, y + 1], (2 * l + 1) % Z, 1)
+                out = jnp.where(pair == l, f, out)
+        zout_e[g] = out
 
     def first(x):
         corr = lax.dot_general(
@@ -357,11 +432,17 @@
                 f = s * rdv[x, y : y + 1]
                 fields[0, g, x + 1, y + 1] = f
 
-    edges = (0, X - 1) if X > 1 else (0,)
-    for x in edges:
+    edges = (0, X - 1)
+    up_first = pos["gx"] < (count["gx"] + 1) // 2
+    xa = jnp.where(up_first, X - 1, 0)
+    for x, turn in ((xa, up_first), (X - 1 - xa, jnp.logical_not(up_first))):
         first(x)
         for g in range(G):
-            send(0, g, ("gx",), (-1 if x == 0 else 1,) if X > 1 else (-1, 1))
+            send(0, g, ("gx",), (1,), turn)
+            send(0, g, ("gx",), (-1,), jnp.logical_not(turn))
+    for g in range(G):
+        pack_edges(g)
+    send_early()
     for x in range(1, X - 1):
         first(x)
     for g in range(G):
@@ -390,23 +471,28 @@
     for k in range(S):
         held, done, ready = {}, [], []
 
-        def begin(g, k=k, held=held, ready=ready):
+        def begin(op, g, k=k, held=held, ready=ready):
+            if op == "E" and k == 0:
+                if "E" not in ready:
+                    ready.append("E")
+                    wait_early()
+                return jnp.where(odd, zin_e[1, g], pltpu.roll(zin_e[0, g], 2, 1))
+            if g // GH not in ready:
+                ready.append(g // GH)
+                wait_yz(k, g // GH)
             if g not in held:
-                if g // GH not in ready:
-                    ready.append(g // GH)
-                    wait_yz(k, g // GH)
-                comb = jnp.where(odd, zin[k, g, 1], pltpu.roll(zin[k, g, 0], 2, 1))
-                held[g] = comb
+                held[g] = jnp.where(odd, zin[k, g, 1], pltpu.roll(zin[k, g, 0], 2, 1))
+            return held[g]
 
         for op, g in ((o[0], int(o[1:])) for o in ORDER[k]):
             if op == "F":
                 forwards(k, g)
                 continue
-            begin(g)
+            comb = begin(op, g)
             if op == "E":
                 wait_x(k, g)
             for x in edges if op == "E" else range(1, X - 1):
-                step(k, g, x, held[g])
+                step(k, g, x, comb)
             done.append(g)
             if k < S - 1:
                 if op == "E":
@@ -436,7 +522,8 @@
     XY = X * Y
     PT = pitch_of(XY)
     f32, bf16 = jnp.float32, jnp.bfloat16
-    rows = C * R // 128 // PL
+    NO = PL // 2 if NY % 2 == 0 else PL
+    rows = C * R // 128 // NO
     NR = max(sum(len(r) for r in RELAYED), 1)
     any_space = pl.BlockSpec(memory_space=pltpu.HBM)
     vmem = pl.BlockSpec(memory_space=pltpu.VMEM)
@@ -459,15 +546,17 @@
             pltpu.VMEM((S, G, X + 2, Y + 2, CG, Z), f32),
             pltpu.VMEM((S, G, CG, Z), f32),
             pltpu.VMEM((S, G, 2, CG, Z), f32),
+            pltpu.VMEM((G, CG, Z), f32),
+            pltpu.VMEM((2, G, CG, Z), f32),
             pltpu.VMEM((NR, Y, CG, Z), f32),
-            pltpu.VMEM((PL, rows, 128), f32),
+            pltpu.VMEM((NO, rows, 128), f32),
             pltpu.VMEM((PL, rows, 128), f32),
             pltpu.VMEM((NZ, rows, 128), f32),
-            pltpu.VMEM((PL, rows, 128), f32),
+            pltpu.VMEM((NO, rows, 128), f32),
             dma((5 + X,)),
             dma((3,)),
             dma((max(PL - 1, 1),)), dma((max(NZ - 1, 1),)), dma((max(PL - 1, 1),)),
-            dma((6,)), dma((S, G, 2)), dma((S, HALVES, 4)),
+            dma((8,)), dma((S, G, 2)), dma((S, HALVES, 4)), dma((4,)),
             dma((1,)), dma((NR,)),
         ],
         compiler_params=pltpu.CompilerParams(

time: 38 us -> 35.4 us (0.932)
  Pallas kernels: 37.8 us -> 35.2 us
    pallas_call x1, Pallas kernels: 36.8 us -> 34.3 us  [body(): pl.pallas_call(functools.partial(kernel, sizes, (C, X, Y, Z, R)), out_sha...]
where the time goes in v3:
time: 35.4 us; the launch traced here: 35.2 us
  Pallas kernels  35.2 us (99%)
    pallas_call x1, Pallas kernels, body(): pl.pallas_call(functools.partial(kernel, sizes, (C, X, Y, Z, R)), out_sha...  34.3 us
    pallas_call x1, Pallas kernels, body(): pl.pallas_call(finish, out_shape=jax.ShapeDtypeStruct((C, XY, Z), f32), i...  0.98 us

profile of v3, /device:TPU:0, one launch (start us, length us, event | category | flops | bytes accessed | tf_op | source)
XLA Modules:
  0.0 35.2 jit_solution(13074127670364465420)
XLA Ops:
  0.0 34.3 %shard_map.64 = f32[2304,128]{1,0:T(8,128)S(1)} custom-call(bf16[2048,128]{1,0:T(8,128)(2,1)} %bitcast.10, bf16[2048,128]{1,0:T(8,128)(2,1)} %bitcast.11, f32[2048,128]{1,0:T(8,128)} %bitcast.9, bf16[8,1024,512]{2,1,0:T(8,128)(2,1)} %bitcast.8, f32[1,512]{1,0:T(1,128)} %bitcast.12, f32[8,8,128]{2,1,0:T(8,128)} %rea_h.1), custom_call_target="tpu_custom_call" | custom-call | tf_op jit(solution)/shard_map/pallas_call | solution.py:531
  34.3 1.0 %shard_map.65 = f32[32,64,128]{2,1,0:T(8,128)} custom-call(f32[32,72,128]{2,1,0:T(8,128)S(1)} %bitcast.7), custom_call_target="tpu_custom_call" | custom-call | tf_op jit(solution)/shard_map/pallas_call | solution.py:573
